TPU v7x, 256 devices: a whole 4x4x8 slice. The times are simulated.
256 devices in a mesh: dp: 16 (over y, x_hi, core), space: 16 (over x_lo, z).
Axes of the slice: x: 4 (x_hi: 2, x_lo: 2; x = x_hi * 2 + x_lo), y: 4, z: 8, core: 2. Of those that a mesh axis runs over, the one named last changes fastest.
Arguments:
- act_in: bfloat16 [16, 32, 64, 2048], P('dp', 'space'), may hold values from -6 to 6
- weight_one: bfloat16 [3, 3, 3, 32, 64], replicated, may hold values from -0.21875 to 0.21875
- bias_one: float32 [64], replicated, may hold values from -3 to 3
- weight_two: bfloat16 [3, 3, 3, 64, 128], replicated, may hold values from -0.15625 to 0.15625
- bias_two: float32 [128], replicated, may hold values from -3 to 3
- cotangent: bfloat16 [16, 16, 32, 4096], P('dp', 'space'), may hold values from -24 to 24
Outputs:
- grad_input: bfloat16 [16, 32, 64, 2048], P('dp', 'space')
- grad_w_one: float32 [3, 3, 3, 32, 64], replicated
- grad_b_one: float32 [64], replicated
- grad_w_two: float32 [3, 3, 3, 64, 128], replicated
- grad_b_two: float32 [128], replicated
All inputs are finite; a program needn't handle non-finite values.
Results may differ from a plain program's by a relative error of at most 0.01.
Values may be sent and summed in bfloat16 or wider, within the bound.
No kernel may reach another device: no remote copies, remote signals or barrier semaphores. Data moves between devices by JAX's collectives and lax.ppermute only.
A program may use at most 128 MiB of HBM per device.

v0:
```python
import math
import jax
import jax.numpy as jnp
from jax import lax
from jax.sharding import PartitionSpec as P


def padded_2(cells, sides, width):
    for axis, dim in sides:
        count = lax.axis_size(axis)
        ends = count - 1
        head = lax.slice_in_dim(cells, 0, width, axis=dim)
        tail = lax.slice_in_dim(cells, cells.shape[dim] - width, cells.shape[dim], axis=dim)
        cells = jnp.concatenate(
            [
                lax.ppermute(tail, axis, [(i, (i + 1) % count) for i in range(ends)]),
                cells,
                lax.ppermute(head, axis, [((i + 1) % count, i) for i in range(ends)]),
            ],
            axis=dim,
        )
    return cells


def forward_conv(padded, kernel):
    return lax.conv_general_dilated(
        padded,
        kernel,
        (1, 1, 1),
        ((0, 0), (1, 1), (1, 1)),
        dimension_numbers=("NDHWC", "DHWIO", "NDHWC"),
        preferred_element_type=jnp.float32,
    )


def weight_grad(padded, delta):
    return lax.conv_general_dilated(
        padded,
        delta,
        (1, 1, 1),
        ((0, 0), (1, 1), (1, 1)),
        dimension_numbers=("CDHWN", "IDHWO", "DHWNC"),
        preferred_element_type=jnp.float32,
    )


def input_grad(delta, kernel, depth_pad):
    return lax.conv_general_dilated(
        delta,
        kernel[::-1, ::-1, ::-1],
        (1, 1, 1),
        (depth_pad, (1, 1), (1, 1)),
        dimension_numbers=("NDHWC", "DHWOI", "NDHWC"),
        preferred_element_type=jnp.float32,
    )


def silu_slope(value):
    sig = jax.nn.sigmoid(value)
    return sig * (1.0 + value * (1.0 - sig))


def local(act_in, weight_one, bias_one, weight_two, bias_two, cotangent):
    samples, slab, side, merged = act_in.shape
    chan_in = weight_one.shape[3]
    chan_mid = weight_one.shape[4]
    chan_out = weight_two.shape[4]
    half = side // 2
    slab_two = slab // 2
    batch_all = samples * lax.axis_size("dp")
    depth_all = slab * lax.axis_size("space")
    scale_one = 16.0 / math.sqrt(batch_all * depth_all * side * side)
    scale_two = 1.0 / math.sqrt(batch_all * (depth_all // 2) * half * half)
    x_pad = padded_2(act_in, (("space", 1),), 1).reshape(samples, slab + 2, side, side, chan_in)
    pre_one = forward_conv(x_pad, weight_one) + bias_one
    act_one = pre_one * jax.nn.sigmoid(pre_one)
    pooled = (
        act_one.reshape(samples, slab_two, 2, half, 2, half, 2, chan_mid)
        .mean(axis=(2, 4, 6))
        .astype(jnp.bfloat16)
    )
    pool_pad = padded_2(
        pooled.reshape(samples, slab_two, half, half * chan_mid), (("space", 1),), 1
    ).reshape(samples, slab_two + 2, half, half, chan_mid)
    pre_two = forward_conv(pool_pad, weight_two) + bias_two
    cot_five = cotangent.reshape(samples, slab_two, half, half, chan_out)
    delta_two = (cot_five.astype(jnp.float32) * silu_slope(pre_two)).astype(jnp.bfloat16)
    gw_two = weight_grad(pool_pad, delta_two)
    gb_two = jnp.sum(delta_two, axis=(0, 1, 2, 3), dtype=jnp.float32)
    gw_two, gb_two = lax.psum((gw_two, gb_two), ("dp", "space"))
    delta_pad = padded_2(
        delta_two.reshape(samples, slab_two, half, half * chan_out), (("space", 1),), 1
    ).reshape(samples, slab_two + 2, half, half, chan_out)
    grad_pooled = input_grad(delta_pad, weight_two, (0, 0))
    spread = jnp.broadcast_to(
        grad_pooled[:, :, None, :, None, :, None, :],
        (samples, slab_two, 2, half, 2, half, 2, chan_mid),
    ).reshape(samples, slab, side, side, chan_mid)
    delta_one = (spread / 8.0 * silu_slope(pre_one)).astype(jnp.bfloat16)
    gw_one = weight_grad(x_pad, delta_one)
    gb_one = jnp.sum(delta_one, axis=(0, 1, 2, 3), dtype=jnp.float32)
    delta_one_pad = padded_2(
        delta_one.reshape(samples, slab, side, side * chan_mid), (("space", 1),), 1
    ).reshape(samples, slab + 2, side, side, chan_mid)
    grad_x = input_grad(delta_one_pad, weight_one, (0, 0))
    gw_one, gb_one = lax.psum((gw_one, gb_one), ("dp", "space"))
    grad_input = grad_x.astype(jnp.bfloat16).reshape(samples, slab, side, side * chan_in)
    return (
        grad_input,
        gw_one * scale_one,
        gb_one * scale_one,
        gw_two * scale_two,
        gb_two * scale_two,
    )


def solution(mesh):
    placed = (P("dp", "space", None, None), P(), P(), P(), P(), P("dp", "space", None, None))
    return jax.shard_map(
        local,
        mesh=mesh,
        in_specs=placed,
        out_specs=(P("dp", "space", None, None), P(), P(), P(), P()),
        check_vma=False,
    )
```

profile of v0, /device:TPU:1, one launch (start us, length us, event | category | flops | bytes accessed | tf_op | source)
XLA Modules:
  0.0 471.9 jit_solution(11770701972416479829)
XLA Ops:
  7.2 1.6 copy.175
  8.9 4.4 collective-permute-start
  13.3 1.3 collective-permute-start.1
  14.6 9.3 %collective-permute-done = bf16[1,1,64,2048]{2,3,1,0:T(8,128)(2,1)S(1)} collective-permute-done((bf16[1,1,64,2048]{2,3,1,0:T(8,128)(2,1)S(1)}, bf16[1,1,64,2048]{2,3,1,0:T(8,128)(2,1)S(1)}, u32[]{:S(2)}, u32[]{:S(2)}) %collective-permute-start) | collective-permute-done | bytes 262176 | tf_op jit(solution)/shard_map/ppermute | solution.py:16
  23.8 4.2 collective-permute-done.1
  28.0 1.7 pad_maximum_fusion
  29.7 1.9 pad
  31.7 6.7 %copy.179 = bf16[4,64,1,8,9,32]{5,3,4,1,0,2:T(8,128)(2,1)} copy(bf16[4,64,1,8,9,32]{1,5,4,3,0,2:T(8,128)(2,1)} %bitcast.114) | data formatting | bytes 2359296 | tf_op jit(solution)/shard_map/conv_general_dilated | solution.py:26
  38.4 1.5 slice.27
  40.0 11.3 %fusion.16 = (f32[2,64,8,9,64]{4,2,3,1,0:T(8,128)S(1)}, f32[2,64,8,9,64]{4,2,3,1,0:T(8,128)}) fusion(f32[64]{0:T(128)S(1)} %copy-done.9, pred[8,9]{0,1:T(8,128)(4,1)S(1)} %copy-done.11, bf16[3,3,3,32,64]{4,3,2,1,0:T(8,128)(2,1)S(1)} %copy-done.7, bf16[4,64,1,7,2,32]{5,3,4,1,0,2:T(8,128)(2,1)S(1)} %slice.27, bf16[4,64,1,8,9,32]{5,3,4,1,0,2:T(8,128)(2,1)} %copy.179), kind=kOutput, calls=%fused_computation.18 | convolution fusion | flops 1018822656 | bytes 6238536 | tf_op jit(solution)/shard_map/conv_general_dilated | solution.py:26
  51.3 0.9 copy.180
  52.2 2.0 slice_reduce_fusion
  54.2 3.3 reduce_sum.36
  57.9 4.2 collective-permute-start.2
  62.3 1.5 collective-permute-start.3
  63.8 5.5 %copy.198 = f32[2,64,8,9,64]{4,1,3,2,0:T(8,128)} copy(f32[2,64,8,9,64]{4,2,3,1,0:T(8,128)} %get-tuple-element.42) | data formatting | bytes 4718592 | tf_op jit(solution)/shard_map/mul | solution.py:60
  69.3 13.0 %copy.205 = bf16[1,4,64,64,32]{4,0,3,2,1:T(2,128)(2,1)} copy(bf16[1,4,64,64,32]{2,4,3,1,0:T(8,128)(2,1)S(1)} %bitcast.106) | data formatting | bytes 2097152 | tf_op jit(solution)/shard_map/reshape | solution.py:74
  82.3 1.2 concatenate.41
  84.7 1.2 concatenate.42
  86.6 0.9 copy.236
  88.2 1.5 add_multiply_fusion.1
  89.9 0.8 convert_reduce_fusion.1
  90.8 4.9 %collective-permute-start.4 = (bf16[1,1,32,4096]{3,2,1,0:T(8,128)(2,1)S(1)}, bf16[1,1,32,4096]{3,2,1,0:T(8,128)(2,1)S(1)}, u32[]{:S(2)}, u32[]{:S(2)}) collective-permute-start(bf16[1,1,32,4096]{3,2,1,0:T(8,128)(2,1)S(1)} %reshape.106), channel_id=1, source_target_pairs={{0,1},{1,2},{2,3},{3,4},{4,5},{5,6},{6,7},{7,8},{8,9},{9,10},{10,1... | collective-permute-start | bytes 786440 | tf_op jit(solution)/shard_map/ppermute | solution.py:16
  95.7 1.7 collective-permute-start.5
  97.4 8.1 %fusion.56 = f32[3,3,3,64,128]{4,3,2,1,0:T(8,128)} fusion(bf16[1,3,32,32,64]{4,0,3,2,1:T(2,128)(2,1)S(1)} %constant_dynamic-update-slice_fusion, bf16[1,1,32,32,128]{4,3,1,2,0:T(8,128)(2,1)S(1)} %get-tuple-element.40), kind=kOutput, calls=%fused_computation.65 | convolution fusion | flops 434307072 | bytes 1540096 | tf_op jit(solution)/shard_map/conv_general_dilated | solution.py:37
  106.6 2.5 fusion.47
  109.3 1.0 broadcast_in_dim.4
  111.1 1.4 copy-done.2
  112.5 1.5 copy.238
  114.0 2.5 reshape.107
  116.5 2.3 fusion.71
  118.8 5.7 %collective-permute-start.6 = (bf16[1,1,64,4096]{3,2,1,0:T(8,128)(2,1)}, bf16[1,1,64,4096]{3,2,1,0:T(8,128)(2,1)}, u32[]{:S(2)}, u32[]{:S(2)}) collective-permute-start(bf16[1,1,64,4096]{3,2,1,0:T(8,128)(2,1)} %get-tuple-element.45), channel_id=1, source_target_pairs={{0,1},{1,2},{2,3},{3,4},{4,5},{5,6},{6,7},{7,8},{8,9},{9,10},{10,1... | collective-permute-start | bytes 1572872 | tf_op jit(solution)/shard_map/ppermute | solution.py:16
  124.5 1.3 collective-permute-start.7
  125.8 66.2 %fusion.18 = f32[3,3,3,32,64]{4,3,2,1,0:T(8,128)} fusion(bf16[1,4,64,64,32]{4,0,3,2,1:T(2,128)(2,1)} %copy.205, bf16[1,2,64,64,64]{4,3,2,1,0:T(8,128)(2,1)S(1)} %bitcast.108), kind=kOutput, calls=%fused_computation.25 | convolution fusion | flops 887193600 | bytes 2318336 | tf_op jit(solution)/shard_map/conv_general_dilated | solution.py:37
  192.0 2.8 convert_reduce_fusion
  194.8 83.0 %all-reduce = (f32[64]{0:T(128)S(1)}, f32[128]{0:T(128)S(1)}) all-reduce(f32[64]{0:T(128)S(1)} %convert_reduce_fusion, f32[128]{0:T(128)S(1)} %copy-done.6), channel_id=1, replica_groups=mesh['dp'=16,'space'=16] {'dp','space'}, use_global_device_ids=true, to_apply=%region_4.0 | all-reduce | flops 192 | bytes 1536 | tf_op jit(solution)/shard_map/psum | solution.py:106
  278.9 2.8 concatenate.34
  281.7 2.8 concatenate.35
  284.4 2.2 maximum_bitcast_fusion
  286.7 2.7 copy.213
  289.4 1.3 pad.6.clone
  290.7 3.0 copy.203
  294.0 18.1 %fusion.4 = bf16[2,64,8,9,32]{4,2,3,1,0:T(8,128)(2,1)} fusion(bf16[3,3,3,32,64]{4,3,2,1,0:T(8,128)(2,1)S(1)} %copy-done.8, bf16[4,64,1,7,2,64]{5,3,4,1,0,2:T(8,128)(2,1)S(1)} %slice.36, bf16[4,64,1,8,9,64]{5,3,4,1,0,2:T(8,128)(2,1)S(1)} %copy.203), kind=kOutput, calls=%fused_computation.6 | convolution fusion | flops 1017249792 | bytes 3518464 | tf_op jit(solution)/shard_map/conv_general_dilated | solution.py:48
  312.1 3.2 copy.204
  315.7 1.1 copy.208
  316.9 143.7 %all-reduce.4.cloned.1.call-done = (f32[3,3,3,32,64]{4,3,2,1,0:T(8,128)}, f32[3,3,3,64,128]{4,3,2,1,0:T(8,128)}) async-done(((f32[3,3,3,32,64]{4,3,2,1,0:T(8,128)}, f32[3,3,3,64,128]{4,3,2,1,0:T(8,128)}), (f32[3,3,3,32,64]{4,3,2,1,0:T(8,128)}, f32[3,3,3,64,128]{4,3,2,1,0:T(8,128)})) %all-reduce.4.cloned.1.call-update) | async-done | bytes 1105936 | tf_op jit(solution)/shard_map/psum | solution.py:106
  460.6 2.2 broadcast_multiply_fusion
  462.8 1.8 broadcast_multiply_fusion.1
  (68 shorter events, 7.1 us)
Async XLA Ops:
  7.2 81.0 %copy-start = (bf16[3,3,3,64,128]{4,3,2,1,0:T(8,128)(2,1)S(1)}, bf16[3,3,3,64,128]{4,3,2,1,0:T(8,128)(2,1)}, u32[]{:S(2)}) copy-start(bf16[3,3,3,64,128]{4,3,2,1,0:T(8,128)(2,1)} %param.9) | copy-start | bytes 1327108
  7.2 453.4 %all-reduce.4.cloned.1.call-start = ((), (), s32[]{:S(2)}) async-start(), calls=%async_computation | async-start | bytes 2654208 | tf_op jit(solution)/shard_map/psum | solution.py:106
  8.8 15.0 %copy-start.3 = (bf16[1,2,64,2048]{2,3,1,0:T(8,128)(2,1)}, bf16[1,2,64,2048]{2,3,1,0:T(8,128)(2,1)S(1)}, u32[]{:S(2)}) copy-start(bf16[1,2,64,2048]{2,3,1,0:T(8,128)(2,1)S(1)} %copy.175) | copy-start | bytes 1572868
  8.9 15.0 %collective-permute-start = (bf16[1,1,64,2048]{2,3,1,0:T(8,128)(2,1)S(1)}, bf16[1,1,64,2048]{2,3,1,0:T(8,128)(2,1)S(1)}, u32[]{:S(2)}, u32[]{:S(2)}) collective-permute-start(bf16[1,1,64,2048]{2,3,1,0:T(8,128)(2,1)S(1)} %get-tuple-element.47), channel_id=1, source_target_pairs={{0,1},{1,2},{2,3},{3,4},{4,5},{5,6},{6,7},{7,8},{8,9},{9,10},{10,1... | collective-permute-start | bytes 786440 | tf_op jit(solution)/shard_map/ppermute | solution.py:16
  13.3 14.7 %collective-permute-start.1 = (bf16[1,1,64,2048]{2,3,1,0:T(8,128)(2,1)S(1)}, bf16[1,1,64,2048]{2,3,1,0:T(8,128)(2,1)S(1)}, u32[]{:S(2)}, u32[]{:S(2)}) collective-permute-start(bf16[1,1,64,2048]{2,3,1,0:T(8,128)(2,1)S(1)} %get-tuple-element.48), channel_id=1, source_target_pairs={{1,0},{2,1},{3,2},{4,3},{5,4},{6,5},{7,6},{8,7},{9,8},{10,9},{11,1... | collective-permute-start | bytes 786440 | tf_op jit(solution)/shard_map/ppermute | solution.py:18
  31.7 8.3 %copy-start.7 = (bf16[3,3,3,32,64]{4,3,2,1,0:T(8,128)(2,1)S(1)}, bf16[3,3,3,32,64]{4,3,2,1,0:T(8,128)(2,1)}, u32[]{:S(2)}) copy-start(bf16[3,3,3,32,64]{4,3,2,1,0:T(8,128)(2,1)} %param.7) | copy-start | bytes 331780
  31.7 8.3 %copy-start.9 = (f32[64]{0:T(128)S(1)}, f32[64]{0:T(128)}, u32[]{:S(2)}) copy-start(f32[64]{0:T(128)} %param.8) | copy-start | bytes 772
  31.7 8.3 %copy-start.11 = (pred[8,9]{0,1:T(8,128)(4,1)S(1)}, pred[8,9]{0,1:T(8,128)(4,1)}, u32[]{:S(2)}) copy-start(pred[8,9]{0,1:T(8,128)(4,1)} %constant.38) | copy-start | bytes 220
  52.2 10.0 %copy-start.4 = (bf16[1,1,32,4096]{3,2,1,0:T(8,128)(2,1)S(1)}, bf16[1,1,32,4096]{3,2,1,0:T(8,128)(2,1)}, u32[]{:S(2)}) copy-start(bf16[1,1,32,4096]{3,2,1,0:T(8,128)(2,1)} %param.11) | copy-start | bytes 786436
  57.9 24.4 %collective-permute-start.2 = (bf16[1,1,32,2048]{3,2,1,0:T(8,128)(2,1)S(1)}, bf16[1,1,32,2048]{3,2,1,0:T(8,128)(2,1)}, u32[]{:S(2)}, u32[]{:S(2)}) collective-permute-start(bf16[1,1,32,2048]{3,2,1,0:T(8,128)(2,1)S(1)} %convert_element_type.57), channel_id=1, source_target_pairs={{0,1},{1,2},{2,3},{3,4},{4,5},{5,6},{6,7},{7,8},{8,9},{9,10},{10,1... | collective-permute-start | bytes 393224 | tf_op jit(solution)/shard_map/ppermute | solution.py:16
  62.3 22.4 %collective-permute-start.3 = (bf16[1,1,32,2048]{3,2,1,0:T(8,128)(2,1)S(1)}, bf16[1,1,32,2048]{3,2,1,0:T(8,128)(2,1)}, u32[]{:S(2)}, u32[]{:S(2)}) collective-permute-start(bf16[1,1,32,2048]{3,2,1,0:T(8,128)(2,1)S(1)} %convert_element_type.57), channel_id=1, source_target_pairs={{1,0},{2,1},{3,2},{4,3},{5,4},{6,5},{7,6},{8,7},{9,8},{10,9},{11,1... | collective-permute-start | bytes 393224 | tf_op jit(solution)/shard_map/ppermute | solution.py:18
  84.7 3.5 copy-start.10
  84.7 3.5 copy-start.12
  90.8 14.6 %collective-permute-start.4 = (bf16[1,1,32,4096]{3,2,1,0:T(8,128)(2,1)S(1)}, bf16[1,1,32,4096]{3,2,1,0:T(8,128)(2,1)S(1)}, u32[]{:S(2)}, u32[]{:S(2)}) collective-permute-start(bf16[1,1,32,4096]{3,2,1,0:T(8,128)(2,1)S(1)} %reshape.106), channel_id=1, source_target_pairs={{0,1},{1,2},{2,3},{3,4},{4,5},{5,6},{6,7},{7,8},{8,9},{9,10},{10,1... | collective-permute-start | bytes 786440 | tf_op jit(solution)/shard_map/ppermute | solution.py:16
  95.7 9.8 %collective-permute-start.5 = (bf16[1,1,32,4096]{3,2,1,0:T(8,128)(2,1)S(1)}, bf16[1,1,32,4096]{3,2,1,0:T(8,128)(2,1)S(1)}, u32[]{:S(2)}, u32[]{:S(2)}) collective-permute-start(bf16[1,1,32,4096]{3,2,1,0:T(8,128)(2,1)S(1)} %reshape.106), channel_id=1, source_target_pairs={{1,0},{2,1},{3,2},{4,3},{5,4},{6,5},{7,6},{8,7},{9,8},{10,9},{11,1... | collective-permute-start | bytes 786440 | tf_op jit(solution)/shard_map/ppermute | solution.py:18
  106.5 3.8 slice-start
  106.6 3.7 slice-start.1
  111.1 1.4 copy-start.2
  118.8 160.1 %collective-permute-start.6 = (bf16[1,1,64,4096]{3,2,1,0:T(8,128)(2,1)}, bf16[1,1,64,4096]{3,2,1,0:T(8,128)(2,1)}, u32[]{:S(2)}, u32[]{:S(2)}) collective-permute-start(bf16[1,1,64,4096]{3,2,1,0:T(8,128)(2,1)} %get-tuple-element.45), channel_id=1, source_target_pairs={{0,1},{1,2},{2,3},{3,4},{4,5},{5,6},{6,7},{7,8},{8,9},{9,10},{10,1... | collective-permute-start | bytes 1572872 | tf_op jit(solution)/shard_map/ppermute | solution.py:16
  124.5 157.2 %collective-permute-start.7 = (bf16[1,1,64,4096]{3,2,1,0:T(8,128)(2,1)}, bf16[1,1,64,4096]{3,2,1,0:T(8,128)(2,1)}, u32[]{:S(2)}, u32[]{:S(2)}) collective-permute-start(bf16[1,1,64,4096]{3,2,1,0:T(8,128)(2,1)} %get-tuple-element.46), channel_id=1, source_target_pairs={{1,0},{2,1},{3,2},{4,3},{5,4},{6,5},{7,6},{8,7},{9,8},{10,9},{11,1... | collective-permute-start | bytes 1572872 | tf_op jit(solution)/shard_map/ppermute | solution.py:18
  125.7 69.1 %copy-start.6 = (f32[128]{0:T(128)S(1)}, f32[128]{0:T(128)}, u32[]{:S(2)}) copy-start(f32[128]{0:T(128)} %get-tuple-element.39) | copy-start | bytes 1540
  290.7 3.3 copy-start.8
  294.0 21.3 %copy-start.5 = (pred[8,9]{1,0:T(8,128)(4,1)S(1)}, pred[8,9]{1,0:T(8,128)(4,1)}, u32[]{:S(2)}) copy-start(pred[8,9]{1,0:T(8,128)(4,1)} %constant.34) | copy-start | bytes 220
  312.1 152.5 %copy-start.1 = (bf16[3,3,3,64,128]{4,3,2,1,0:T(8,128)(2,1)S(1)}, bf16[3,3,3,64,128]{4,3,2,1,0:T(8,128)(2,1)}, u32[]{:S(2)}) copy-start(bf16[3,3,3,64,128]{4,3,2,1,0:T(8,128)(2,1)} %param.9) | copy-start | bytes 1327108
Sparse Core Ops, SparseCore 0:
  194.9 265.5 all-reduce.3
where the time goes:
time: 481 us; the launch traced here: 472 us
  waiting for transfers between devices  157 us (33%)
  matrix products  108 us (22%)
  blocking collectives  83 us (17%)
  local copies, waits for them, and re-layouts  64.9 us (13%)
  starting transfers between devices  25 us (5%)
  other arithmetic  19.1 us (4%)
  between operations  15 us (3%)
    psum x1, waiting for transfers between devices, local(): gw_one, gb_one = lax.psum((gw_one, gb_one), ('dp', 'space'))  144 us
    psum x1, blocking collectives, local(): gw_one, gb_one = lax.psum((gw_one, gb_one), ('dp', 'space'))  83 us
    conv_general_dilated x2, matrix products, weight_grad(): lax.conv_general_dilated(padded, delta, (1, 1, 1), ((0, 0), (1, 1), (1, 1...  74.3 us
    conv_general_dilated x2, matrix products, input_grad(): lax.conv_general_dilated(delta, kernel[::-1, ::-1, ::-1], (1, 1, 1), (dep...  20.6 us
    ppermute x4, starting transfers between devices, padded_2(): lax.ppermute(tail, axis, [(i, (i + 1) % count) for i in range(ends)])  19.2 us
    reshape x2, local copies, waits for them, and re-layouts, local(): padded_2(act_in, (('space', 1),), 1)  15 us
    conv_general_dilated x2, matrix products, forward_conv(): lax.conv_general_dilated(padded, kernel, (1, 1, 1), ((0, 0), (1, 1), (1,...  12.8 us
    concatenate x8, local copies, waits for them, and re-layouts, padded_2(): jnp.concatenate([lax.ppermute(tail, axis, [(i, (i + 1) % count) for i in...  10.2 us
  transfers between devices with their start and end apart: 9, of which 3 were waited for; matrix products, arithmetic and copies ran while one was open for 29% of the time, Pallas kernels for 0%

commit v1 on v0

--- a/solution.py
+++ b/solution.py
@@ -103,7 +103,7 @@
         delta_one.reshape(samples, slab, side, side * chan_mid), (("space", 1),), 1
     ).reshape(samples, slab + 2, side, side, chan_mid)
     grad_x = input_grad(delta_one_pad, weight_one, (0, 0))
-    gw_one, gb_one = lax.psum((gw_one, gb_one), ("dp", "space"))
+    gw_one, gb_one = jax.lax.psum(jax.lax.psum((gw_one, gb_one), "space"), "dp")
     grad_input = grad_x.astype(jnp.bfloat16).reshape(samples, slab, side, side * chan_in)
     return (
         grad_input,

time: 481 us -> 865 us (1.80)
  waiting for transfers between devices: 157 us -> 459 us
  blocking collectives: 83 us -> 152 us
  matrix products: 108 us -> 125 us
    psum x1 -> x3, waiting for transfers between devices: 144 us -> 445 us  [the longest x1 269 us: local(): gw_two, gb_two = lax.psum((gw_two, gb_two), ('dp', 'space'))]
    psum x1 -> x3, blocking collectives: 83 us -> 152 us  [the longest x1 82.1 us: local(): gw_two, gb_two = lax.psum((gw_two, gb_two), ('dp', 'space'))]
    conv_general_dilated x2, matrix products: 74.3 us -> 91.8 us  [weight_grad(): lax.conv_general_dilated(padded, delta, (1, 1, 1), ((0, 0), (1, 1), (1, 1...]
  transfers between devices with their start and end apart: 9 -> 11, of which waited for: 3 -> 5; matrix products, arithmetic and copies ran while one was open for 29% -> 5% of each run, Pallas kernels for 0% -> 0%
where the time goes in v1:
time: 865 us; the launch traced here: 857 us
  waiting for transfers between devices  459 us (53%)
  blocking collectives  152 us (18%)
  matrix products  125 us (14%)
  local copies, waits for them, and re-layouts  63.9 us (7%)
  starting transfers between devices  23.9 us (3%)
  other arithmetic  18.7 us (2%)
  between operations  14.6 us (2%)
    psum x1, waiting for transfers between devices, local(): gw_two, gb_two = lax.psum((gw_two, gb_two), ('dp', 'space'))  269 us
    psum x2, waiting for transfers between devices, local(): gw_one, gb_one = jax.lax.psum(jax.lax.psum((gw_one, gb_one), 'space'), 'dp')  177 us
    conv_general_dilated x2, matrix products, weight_grad(): lax.conv_general_dilated(padded, delta, (1, 1, 1), ((0, 0), (1, 1), (1, 1...  91.8 us
    psum x1, blocking collectives, local(): gw_two, gb_two = lax.psum((gw_two, gb_two), ('dp', 'space'))  82.1 us
    psum x2, blocking collectives, local(): gw_one, gb_one = jax.lax.psum(jax.lax.psum((gw_one, gb_one), 'space'), 'dp')  69.5 us
    conv_general_dilated x2, matrix products, input_grad(): lax.conv_general_dilated(delta, kernel[::-1, ::-1, ::-1], (1, 1, 1), (dep...  20.5 us
    ppermute x4, starting transfers between devices, padded_2(): lax.ppermute(tail, axis, [(i, (i + 1) % count) for i in range(ends)])  18 us
  transfers between devices with their start and end apart: 11, of which 5 were waited for; matrix products, arithmetic and copies ran while one was open for 5% of the time, Pallas kernels for 0%

profile of v1, /device:TPU:1, one launch (start us, length us, event | category | flops | bytes accessed | tf_op | source)
XLA Modules:
  0.0 856.6 jit_solution(4533102890034049058)
XLA Ops:
  7.2 1.6 copy.175
  8.9 4.4 collective-permute-start
  13.3 1.3 collective-permute-start.1
  14.6 9.3 %collective-permute-done = bf16[1,1,64,2048]{2,3,1,0:T(8,128)(2,1)S(1)} collective-permute-done((bf16[1,1,64,2048]{2,3,1,0:T(8,128)(2,1)S(1)}, bf16[1,1,64,2048]{2,3,1,0:T(8,128)(2,1)S(1)}, u32[]{:S(2)}, u32[]{:S(2)}) %collective-permute-start) | collective-permute-done | bytes 262176 | tf_op jit(solution)/shard_map/ppermute | solution.py:16
  23.8 4.2 collective-permute-done.1
  28.0 1.7 pad_maximum_fusion
  29.7 1.9 pad
  31.7 6.8 copy.179
  38.4 1.5 slice.27
  40.0 11.3 %fusion.16 = (f32[2,64,8,9,64]{4,2,3,1,0:T(8,128)S(1)}, f32[2,64,8,9,64]{4,2,3,1,0:T(8,128)}) fusion(f32[64]{0:T(128)S(1)} %copy-done.8, pred[8,9]{0,1:T(8,128)(4,1)S(1)} %copy-done.11, bf16[3,3,3,32,64]{4,3,2,1,0:T(8,128)(2,1)S(1)} %copy-done.6, bf16[4,64,1,7,2,32]{5,3,4,1,0,2:T(8,128)(2,1)S(1)} %slice.27, bf16[4,64,1,8,9,32]{5,3,4,1,0,2:T(8,128)(2,1)} %copy.179), kind=kOutput, calls=%fused_computation.18 | convolution fusion | flops 1018822656 | bytes 6238536 | tf_op jit(solution)/shard_map/conv_general_dilated | solution.py:26
  52.2 2.0 slice_reduce_fusion
  54.2 3.3 reduce_sum.36
  58.0 4.2 collective-permute-start.2
  62.3 1.8 collective-permute-start.3
  64.1 5.4 copy.198
  69.5 13.0 %copy.205 = bf16[1,4,64,64,32]{4,0,3,2,1:T(2,128)(2,1)} copy(bf16[1,4,64,64,32]{2,4,3,1,0:T(8,128)(2,1)S(1)} %bitcast.106) | data formatting | bytes 2097152 | tf_op jit(solution)/shard_map/reshape | solution.py:74
  82.5 1.2 concatenate.41
  84.9 1.2 concatenate.42
  88.4 1.5 add_multiply_fusion.1
  90.5 4.9 collective-permute-start.4
  95.4 1.5 collective-permute-start.5
  96.9 8.1 fusion.56
  104.9 82.1 %psum.47 = f32[128]{0:T(128)} all-reduce(f32[128]{0:T(128)S(1)} %get-tuple-element.35), channel_id=1, replica_groups=mesh['dp'=16,'space'=16] {'dp','space'}, use_global_device_ids=true, to_apply=%region_9.10 | all-reduce | flops 128 | bytes 1024 | tf_op jit(solution)/shard_map/psum | solution.py:90
  188.2 2.5 fusion.47
  192.7 1.4 copy-done.2
  194.1 1.4 copy.238
  195.5 83.7 %fusion.18 = f32[3,3,3,32,64]{4,3,2,1,0:T(8,128)} fusion(bf16[1,4,64,64,32]{4,0,3,2,1:T(2,128)(2,1)S(1)} %bitcast.116, bf16[1,2,64,64,64]{4,3,2,1,0:T(8,128)(2,1)S(1)} %bitcast.108), kind=kOutput, calls=%fused_computation.25 | convolution fusion | flops 887193600 | bytes 2318336 | tf_op jit(solution)/shard_map/conv_general_dilated | solution.py:37
  280.0 2.5 reshape.107
  282.5 2.3 fusion.71
  284.8 4.5 collective-permute-start.6
  289.2 1.3 collective-permute-start.7
  290.5 2.8 convert_reduce_fusion
  293.3 30.4 %psum.44 = f32[64]{0:T(128)S(1)} all-reduce(f32[64]{0:T(128)S(1)} %convert_reduce_fusion), channel_id=1, replica_groups=mesh['dp'=16,'space'=16] {'space'}, use_global_device_ids=true, to_apply=%region_5.0 | all-reduce | flops 64 | bytes 512 | tf_op jit(solution)/shard_map/psum | solution.py:106
  323.7 39.1 %psum.45 = f32[64]{0:T(128)S(1)} all-reduce(f32[64]{0:T(128)S(1)} %psum.44), channel_id=1, replica_groups=mesh['dp'=16,'space'=16] {'dp'}, use_global_device_ids=true, to_apply=%region_6.0 | all-reduce | flops 64 | bytes 512 | tf_op jit(solution)/shard_map/psum | solution.py:106
  363.4 36.3 %all-reduce.4.cloned.1.call-done = f32[3,3,3,32,64]{4,3,2,1,0:T(8,128)} async-done(((f32[3,3,3,32,64]{4,3,2,1,0:T(8,128)}), f32[3,3,3,32,64]{4,3,2,1,0:T(8,128)}) %all-reduce.4.cloned.1.call-update) | async-done | bytes 221200 | tf_op jit(solution)/shard_map/psum | solution.py:106
  399.7 268.8 %all-reduce.8.cloned.1.call-done = f32[3,3,3,64,128]{4,3,2,1,0:T(8,128)} async-done(((f32[3,3,3,64,128]{4,3,2,1,0:T(8,128)}), f32[3,3,3,64,128]{4,3,2,1,0:T(8,128)}) %all-reduce.8.cloned.1.call-update) | async-done | bytes 884752 | tf_op jit(solution)/shard_map/psum | solution.py:90
  668.4 2.2 broadcast_multiply_fusion
  670.6 140.2 %all-reduce.6.cloned.1.call-done = f32[3,3,3,32,64]{4,3,2,1,0:T(8,128)} async-done(((f32[3,3,3,32,64]{4,3,2,1,0:T(8,128)}), f32[3,3,3,32,64]{4,3,2,1,0:T(8,128)}) %all-reduce.6.cloned.1.call-update) | async-done | bytes 221200 | tf_op jit(solution)/shard_map/psum | solution.py:106
  810.8 1.8 broadcast_multiply_fusion.1
  812.7 2.8 concatenate.34
  815.4 2.1 concatenate.35
  817.5 2.2 maximum_bitcast_fusion
  819.8 2.7 copy.213
  822.5 1.3 pad.6.clone
  823.8 3.0 copy.203
  827.1 18.0 %fusion.4 = bf16[2,64,8,9,32]{4,2,3,1,0:T(8,128)(2,1)} fusion(bf16[3,3,3,32,64]{4,3,2,1,0:T(8,128)(2,1)S(1)} %copy-done.7, bf16[4,64,1,7,2,64]{5,3,4,1,0,2:T(8,128)(2,1)S(1)} %slice.36, bf16[4,64,1,8,9,64]{5,3,4,1,0,2:T(8,128)(2,1)S(1)} %copy.203), kind=kOutput, calls=%fused_computation.6 | convolution fusion | flops 1017249792 | bytes 3518464 | tf_op jit(solution)/shard_map/conv_general_dilated | solution.py:48
  845.2 3.2 copy.204
  848.7 1.1 copy.208
  (81 shorter events, 10.6 us)
Async XLA Ops:
  7.2 81.2 %copy-start = (bf16[3,3,3,64,128]{4,3,2,1,0:T(8,128)(2,1)S(1)}, bf16[3,3,3,64,128]{4,3,2,1,0:T(8,128)(2,1)}, u32[]{:S(2)}) copy-start(bf16[3,3,3,64,128]{4,3,2,1,0:T(8,128)(2,1)} %param.9) | copy-start | bytes 1327108
  7.2 392.5 %all-reduce.4.cloned.1.call-start = ((), (), s32[]{:S(2)}) async-start(), calls=%async_computation | async-start | bytes 884736 | tf_op jit(solution)/shard_map/psum | solution.py:106
  8.8 15.0 %copy-start.3 = (bf16[1,2,64,2048]{2,3,1,0:T(8,128)(2,1)}, bf16[1,2,64,2048]{2,3,1,0:T(8,128)(2,1)S(1)}, u32[]{:S(2)}) copy-start(bf16[1,2,64,2048]{2,3,1,0:T(8,128)(2,1)S(1)} %copy.175) | copy-start | bytes 1572868
  8.9 15.0 %collective-permute-start = (bf16[1,1,64,2048]{2,3,1,0:T(8,128)(2,1)S(1)}, bf16[1,1,64,2048]{2,3,1,0:T(8,128)(2,1)S(1)}, u32[]{:S(2)}, u32[]{:S(2)}) collective-permute-start(bf16[1,1,64,2048]{2,3,1,0:T(8,128)(2,1)S(1)} %get-tuple-element.43), channel_id=1, source_target_pairs={{0,1},{1,2},{2,3},{3,4},{4,5},{5,6},{6,7},{7,8},{8,9},{9,10},{10,1... | collective-permute-start | bytes 786440 | tf_op jit(solution)/shard_map/ppermute | solution.py:16
  13.3 14.7 %collective-permute-start.1 = (bf16[1,1,64,2048]{2,3,1,0:T(8,128)(2,1)S(1)}, bf16[1,1,64,2048]{2,3,1,0:T(8,128)(2,1)S(1)}, u32[]{:S(2)}, u32[]{:S(2)}) collective-permute-start(bf16[1,1,64,2048]{2,3,1,0:T(8,128)(2,1)S(1)} %get-tuple-element.44), channel_id=1, source_target_pairs={{1,0},{2,1},{3,2},{4,3},{5,4},{6,5},{7,6},{8,7},{9,8},{10,9},{11,1... | collective-permute-start | bytes 786440 | tf_op jit(solution)/shard_map/ppermute | solution.py:18
  31.7 8.3 copy-start.6
  31.7 8.3 copy-start.8
  31.7 8.3 copy-start.11
  52.2 10.0 %copy-start.4 = (bf16[1,1,32,4096]{3,2,1,0:T(8,128)(2,1)S(1)}, bf16[1,1,32,4096]{3,2,1,0:T(8,128)(2,1)}, u32[]{:S(2)}) copy-start(bf16[1,1,32,4096]{3,2,1,0:T(8,128)(2,1)} %param.11) | copy-start | bytes 786436
  58.0 24.5 %collective-permute-start.2 = (bf16[1,1,32,2048]{3,2,1,0:T(8,128)(2,1)S(1)}, bf16[1,1,32,2048]{3,2,1,0:T(8,128)(2,1)}, u32[]{:S(2)}, u32[]{:S(2)}) collective-permute-start(bf16[1,1,32,2048]{3,2,1,0:T(8,128)(2,1)S(1)} %convert_element_type.57), channel_id=1, source_target_pairs={{0,1},{1,2},{2,3},{3,4},{4,5},{5,6},{6,7},{7,8},{8,9},{9,10},{10,1... | collective-permute-start | bytes 393224 | tf_op jit(solution)/shard_map/ppermute | solution.py:16
  62.3 22.6 %collective-permute-start.3 = (bf16[1,1,32,2048]{3,2,1,0:T(8,128)(2,1)S(1)}, bf16[1,1,32,2048]{3,2,1,0:T(8,128)(2,1)}, u32[]{:S(2)}, u32[]{:S(2)}) collective-permute-start(bf16[1,1,32,2048]{3,2,1,0:T(8,128)(2,1)S(1)} %convert_element_type.57), channel_id=1, source_target_pairs={{1,0},{2,1},{3,2},{4,3},{5,4},{6,5},{7,6},{8,7},{9,8},{10,9},{11,1... | collective-permute-start | bytes 393224 | tf_op jit(solution)/shard_map/ppermute | solution.py:18
  84.9 3.5 copy-start.9
  84.9 3.5 copy-start.12
  90.5 96.5 %collective-permute-start.4 = (bf16[1,1,32,4096]{3,2,1,0:T(8,128)(2,1)S(1)}, bf16[1,1,32,4096]{3,2,1,0:T(8,128)(2,1)S(1)}, u32[]{:S(2)}, u32[]{:S(2)}) collective-permute-start(bf16[1,1,32,4096]{3,2,1,0:T(8,128)(2,1)S(1)} %reshape.106), channel_id=1, source_target_pairs={{0,1},{1,2},{2,3},{3,4},{4,5},{5,6},{6,7},{7,8},{8,9},{9,10},{10,1... | collective-permute-start | bytes 786440 | tf_op jit(solution)/shard_map/ppermute | solution.py:16
  95.4 91.7 %collective-permute-start.5 = (bf16[1,1,32,4096]{3,2,1,0:T(8,128)(2,1)S(1)}, bf16[1,1,32,4096]{3,2,1,0:T(8,128)(2,1)S(1)}, u32[]{:S(2)}, u32[]{:S(2)}) collective-permute-start(bf16[1,1,32,4096]{3,2,1,0:T(8,128)(2,1)S(1)} %reshape.106), channel_id=1, source_target_pairs={{1,0},{2,1},{3,2},{4,3},{5,4},{6,5},{7,6},{8,7},{9,8},{10,9},{11,1... | collective-permute-start | bytes 786440 | tf_op jit(solution)/shard_map/ppermute | solution.py:18
  188.0 3.8 slice-start
  188.2 3.7 slice-start.1
  190.7 4.8 slice-start.2
  191.9 3.6 slice-start.3
  192.7 1.4 copy-start.2
  195.5 83.8 %copy-start.10 = (f32[128]{0:T(128)S(1)}, f32[128]{0:T(128)}, u32[]{:S(2)}) copy-start(f32[128]{0:T(128)} %psum.47) | copy-start | bytes 1540
  279.2 389.2 %all-reduce.8.cloned.1.call-start = ((), (), s32[]{:S(2)}) async-start(), calls=%async_computation.2 | async-start | bytes 1769472 | tf_op jit(solution)/shard_map/psum | solution.py:90
  280.0 530.9 %all-reduce.6.cloned.1.call-start = ((), (), s32[]{:S(2)}) async-start(), calls=%async_computation.1 | async-start | bytes 884736 | tf_op jit(solution)/shard_map/psum | solution.py:106
  284.8 527.9 %collective-permute-start.6 = (bf16[1,1,64,4096]{3,2,1,0:T(8,128)(2,1)}, bf16[1,1,64,4096]{3,2,1,0:T(8,128)(2,1)}, u32[]{:S(2)}, u32[]{:S(2)}) collective-permute-start(bf16[1,1,64,4096]{3,2,1,0:T(8,128)(2,1)} %get-tuple-element.41), channel_id=1, source_target_pairs={{0,1},{1,2},{2,3},{3,4},{4,5},{5,6},{6,7},{7,8},{8,9},{9,10},{10,1... | collective-permute-start | bytes 1572872 | tf_op jit(solution)/shard_map/ppermute | solution.py:16
  289.2 526.2 %collective-permute-start.7 = (bf16[1,1,64,4096]{3,2,1,0:T(8,128)(2,1)}, bf16[1,1,64,4096]{3,2,1,0:T(8,128)(2,1)S(1)}, u32[]{:S(2)}, u32[]{:S(2)}) collective-permute-start(bf16[1,1,64,4096]{3,2,1,0:T(8,128)(2,1)} %get-tuple-element.42), channel_id=1, source_target_pairs={{1,0},{2,1},{3,2},{4,3},{5,4},{6,5},{7,6},{8,7},{9,8},{10,9},{11,1... | collective-permute-start | bytes 1572872 | tf_op jit(solution)/shard_map/ppermute | solution.py:18
  823.7 3.3 copy-start.7
  827.1 21.2 %copy-start.5 = (pred[8,9]{1,0:T(8,128)(4,1)S(1)}, pred[8,9]{1,0:T(8,128)(4,1)}, u32[]{:S(2)}) copy-start(pred[8,9]{1,0:T(8,128)(4,1)} %constant.34) | copy-start | bytes 220
  827.1 22.8 %copy-start.1 = (bf16[3,3,3,64,128]{4,3,2,1,0:T(8,128)(2,1)S(1)}, bf16[3,3,3,64,128]{4,3,2,1,0:T(8,128)(2,1)}, u32[]{:S(2)}) copy-start(bf16[3,3,3,64,128]{4,3,2,1,0:T(8,128)(2,1)} %param.9) | copy-start | bytes 1327108
Sparse Core Ops, SparseCore 0:
  279.3 120.2 all-reduce.3
  405.7 262.6 all-reduce.7
  671.1 139.7 all-reduce.5
